TPU v7x, 512 devices: a whole 4x8x8 slice. The times are simulated.
512 devices in a mesh: shot: 64 (over x, y, core), det: 8 (over z).
Axes of the slice: x: 4, y: 8, z: 8, core: 2. Of those that a mesh axis runs over, the one named last changes fastest.
Arguments:
- events: int32 [65536, 8192], P('shot', 'det'), may hold values from 0 to 1, as said below
- pair_patches: int32 [8, 26, 2], P('det'), may hold values from 0 to 7, as said below
- pair_owners: int32 [8, 26, 2], P('det'), may hold values from 0 to 63, as said below
- triples: int32 [8, 256, 3], P('det'), may hold values from 0 to 1023, as said below
Outputs:
- intra_rates: float32 [64, 128, 128], P('det', 'shot')
- boundary_rates: float32 [8, 64, 2, 128, 128], P('det', 'shot')
- detector_load: float32 [64, 128], P(None, 'shot')
- triple_cumulant: float32 [8, 256], P('det')
Inputs may be any that keep to these rules, and one draw needn't show every extreme that they name: events[s, i] is 1 where detector i fired in shot s, else 0. `pair_patches`: row d lists 26 blocks of panel d, each naming two different patches of the panel; no two blocks name the same two patches. `pair_owners`: of the 52 owner entries of one panel, no shot index is named more than 2 times, and in every panel some index is named exactly 2 times. `triples`: each triple holds three different detector indices of the panel in increasing order.
All inputs are finite; a program needn't handle non-finite values.
Results may differ from a plain program's by a relative error of at most 0.0003.
Values sent between devices are 32-bit elements; how exact they have to be, the bound alone decides.
No kernel may reach another device: no remote copies, remote signals or barrier semaphores. Data moves between devices by JAX's collectives and lax.ppermute only.
A program may use at most 64 MiB of HBM per device.

v0:
```python
import jax
import jax.numpy as jnp
from jax import lax
from jax.sharding import Mesh
from jax.sharding import PartitionSpec as P

PB = 128
SHOT = ("shot_0", "shot_1", "shot_2")


def split_up(x, dim, count):
    before, after = (x.shape[:dim], x.shape[dim + 1 :])
    return jnp.moveaxis(x.reshape(*before, count, -1, *after), dim, 0)


def sum_at_owner(x, axis, dim):
    tiles = split_up(x, dim, lax.axis_size(axis))
    arrived = lax.all_to_all(tiles, axis, split_axis=0, concat_axis=0, tiled=True)
    return arrived.sum(axis=0)


def by_axis(x, axes):
    for axis in axes:
        x = lax.psum(x, axis)
    return x


def laid_out(tiles, dim):
    tiles = jnp.moveaxis(tiles, 0, dim)
    dims = tiles.shape
    return tiles.reshape(*dims[:dim], dims[dim] * dims[dim + 1], *dims[dim + 2 :])


def sent_to_all(x, axis):
    copies = jnp.broadcast_to(x, (lax.axis_size(axis), *x.shape))
    return lax.all_to_all(copies, axis, split_axis=0, concat_axis=0, tiled=True)


def gather_directly(x, axis, dim):
    return laid_out(sent_to_all(x, axis), dim)


def fit_rates(coincide, row_count, col_count, shot_total):
    inverse = 1.0 / shot_total
    joint_rate = coincide * inverse
    row_rate = row_count[..., :, None] * inverse
    col_rate = col_count[..., None, :] * inverse
    denominator = jnp.maximum(1.0 - 2.0 * row_rate - 2.0 * col_rate + 4.0 * joint_rate, 0.25)
    excess = (joint_rate - row_rate * col_rate) / denominator
    return 100.0 * (0.5 - 0.5 * jnp.sqrt(jnp.maximum(1.0 - 4.0 * excess, 0.04)))


def route_table(owner_row, shot_count, recv_slots):
    owner_ids = jnp.arange(shot_count, dtype=jnp.int32)
    hit = owner_row[None, :] == owner_ids[:, None]
    rank = jnp.cumsum(hit.astype(jnp.int32), axis=1) - 1
    slot_ids = jnp.arange(recv_slots, dtype=jnp.int32)
    chosen = hit[:, None, :] & (rank[:, None, :] == slot_ids[None, :, None])
    entry_pair = jnp.arange(owner_row.shape[0], dtype=jnp.int32) // 2
    pair_slot = jnp.sum(jnp.where(chosen, entry_pair[None, None, :], 0), axis=2)
    valid = jnp.any(chosen, axis=2).astype(jnp.float32)
    return (pair_slot, valid)


def local(events, pair_patches, pair_owners, triples):
    shot_dev, det_dev = events.shape
    shot_count = lax.axis_size(SHOT)
    shot_index = lax.axis_index(SHOT)
    shot_total = float(shot_dev * shot_count)
    inverse = 1.0 / shot_total
    patch_dev = det_dev // PB
    rows_own = PB // shot_count
    pair_count = pair_patches.shape[1]
    triple_count = triples.shape[1]
    recv_slots = max(2, 4 * pair_count // shot_count)
    bit_matrix = events.astype(jnp.bfloat16)
    patches = bit_matrix.reshape(shot_dev, patch_dev, PB)
    local_counts = jnp.sum(events, axis=0).astype(jnp.float32)
    triple_index = triples[0]
    picked = (
        jnp.take(events, triple_index.reshape(-1), axis=1)
        .astype(jnp.float32)
        .reshape(shot_dev, triple_count, 3)
    )
    first_bit = picked[:, :, 0]
    second_bit = picked[:, :, 1]
    third_bit = picked[:, :, 2]
    triple_terms = jnp.stack(
        [
            jnp.sum(first_bit * second_bit, axis=0),
            jnp.sum(first_bit * third_bit, axis=0),
            jnp.sum(second_bit * third_bit, axis=0),
            jnp.sum(first_bit * second_bit * third_bit, axis=0),
        ]
    )
    intra = jnp.einsum("sai,saj->aij", patches, patches, preferred_element_type=jnp.float32)
    pair_ends = pair_patches[0]
    first_columns = jnp.take(patches, pair_ends[:, 0], axis=1)
    second_columns = jnp.take(patches, pair_ends[:, 1], axis=1)
    cross = jnp.einsum(
        "spi,spj->pij", first_columns, second_columns, preferred_element_type=jnp.float32
    )
    joined = sum_at_owner(jnp.concatenate([intra, cross], axis=0), SHOT, 1)
    intra_share = joined[:patch_dev]
    pair_share = joined[patch_dev:]
    counts, triple_total = (by_axis(local_counts, SHOT), by_axis(triple_terms, SHOT))
    patch_counts = counts.reshape(patch_dev, PB)
    row_counts = lax.dynamic_slice_in_dim(patch_counts, shot_index * rows_own, rows_own, 1)
    intra_rates = fit_rates(intra_share, row_counts, patch_counts, shot_total)
    load_share = jnp.sum(intra_rates, axis=2)
    detector_load = gather_directly(load_share, "det", 0)
    pair_slot, valid = route_table(pair_owners[0].reshape(-1), shot_count, recv_slots)
    fitted = fit_rates(
        pair_share,
        jnp.take(row_counts, pair_ends[:, 0], axis=0),
        jnp.take(patch_counts, pair_ends[:, 1], axis=0),
        shot_total,
    )
    outgoing = jnp.take(fitted, pair_slot.reshape(-1), axis=0).reshape(
        shot_count, recv_slots, rows_own, PB
    )
    outgoing = outgoing * valid[:, :, None, None]
    incoming = lax.all_to_all(outgoing, SHOT, split_axis=0, concat_axis=2, tiled=True)
    boundary = incoming.reshape(recv_slots, PB, PB)
    moments = triple_total * inverse
    means = jnp.take(counts, triple_index.reshape(-1), axis=0).reshape(triple_count, 3) * inverse
    mean_first = means[:, 0]
    mean_second = means[:, 1]
    mean_third = means[:, 2]
    kappa = (
        moments[3]
        - moments[0] * mean_third
        - moments[1] * mean_second
        - moments[2] * mean_first
        + 2.0 * mean_first * mean_second * mean_third
    )
    triple_cumulant = 1000.0 * kappa
    return (intra_rates, boundary[None, None], detector_load, triple_cumulant[None])


def solution(mesh):
    torus = Mesh(
        mesh.devices.reshape(4, 8, 2, mesh.shape["det"]), ("shot_0", "shot_1", "shot_2", "det")
    )
    return jax.shard_map(
        local,
        mesh=torus,
        in_specs=(P(SHOT, "det"), P("det", None, None), P("det", None, None), P("det", None, None)),
        out_specs=(
            P("det", SHOT, None),
            P("det", SHOT, None, None, None),
            P(None, SHOT),
            P("det", None),
        ),
        check_vma=False,
    )
```

profile of v0, /device:TPU:1, one launch (start us, length us, event | category | flops | bytes accessed | tf_op | source)
XLA Modules:
  0.0 155.3 jit_solution(5718766093984803097)
XLA Ops:
  0.6 5.4 %copy.90 = s32[1024,1024]{0,1:T(8,128)} copy(s32[1024,1024]{1,0:T(8,128)} %param.6) | data formatting | bytes 8388608 | tf_op args[0]
  6.0 2.8 %convert_element_type.24 = bf16[1024,1024]{0,1:T(8,128)(2,1)S(1)} convert(s32[1024,1024]{0,1:T(8,128)} %copy.90) | non-fusion elementwise | flops 1048576 | bytes 6291456 | tf_op jit(solution)/shard_map/convert_element_type | solution.py:76
  8.8 1.3 copy-done
  10.1 0.7 fusion.24
  10.8 3.0 %copy.92 = bf16[1024,8,128]{2,0,1:T(8,128)(2,1)S(1)} copy(bf16[1024,8,128]{0,2,1:T(8,128)(2,1)} %bitcast.87) | data formatting | bytes 4194304 | tf_op jit(solution)/shard_map/reshape | solution.py:77
  13.9 4.5 %gather_fusion.6 = bf16[26,1024,128]{2,1,0:T(8,128)(2,1)} fusion(bf16[1024,8,128]{2,0,1:T(8,128)(2,1)S(1)} %copy.92, s32[1024]{0:T(1024)S(1)} %get-tuple-element.40), kind=kCustom, calls=%fused_computation.1.clone | custom fusion | bytes 13631592 | tf_op jit(solution)/shard_map/jit(_take)/gather | solution.py:99
  18.5 4.6 %gather_fusion.5 = bf16[26,1024,128]{2,1,0:T(8,128)(2,1)} fusion(bf16[1024,8,128]{2,0,1:T(8,128)(2,1)S(1)} %copy.92, s32[1024]{0:T(1024)S(1)} %get-tuple-element.41), kind=kCustom, calls=%fused_computation.clone | custom fusion | bytes 13631592 | tf_op jit(solution)/shard_map/jit(_take)/gather | solution.py:98
  23.1 7.4 %fusion = f32[26,128,128]{2,1,0:T(8,128)S(1)} fusion(bf16[26,1024,128]{2,1,0:T(8,128)(2,1)} %gather_fusion.6, bf16[26,1024,128]{2,1,0:T(8,128)(2,1)} %gather_fusion.5, pred[26]{0:T(512)(128)(4,1)S(1)} %get-tuple-element.36, pred[26]{0:T(512)(128)(4,1)S(1)} %get-tuple-element.22), kind=kOutput, calls=%fused_computation.7 | convolution fusion | flops 879230976 | bytes 15335476 | tf_op jit(solution)/shard_map/spi,spj->pij/dot_general | solution.py:100
  30.7 2.1 %copy.115 = f32[34,64,2,128]{3,2,0,1:T(2,128)} copy(f32[34,64,2,128]{3,2,1,0:T(2,128)S(1)} %bitcast.89) | data formatting | bytes 4456448 | tf_op jit(solution)/shard_map/reshape | solution.py:13
  32.8 11.8 %all-to-all-start = ((f32[64,34,2,128]{3,2,1,0:T(2,128)}), f32[64,34,2,128]{3,2,1,0:T(2,128)}, u32[]{:S(2)}, u32[]{:S(2)}) async-start(f32[64,34,2,128]{3,2,1,0:T(2,128)} %bitcast.83), calls=%async_computation | async-start | bytes 4456448 | tf_op jit(solution)/shard_map/all_to_all | solution.py:18
  44.6 2.5 %reduce_sum.73 = s32[1024]{0:T(1024)S(1)} reduce(s32[1024,1024]{1,0:T(8,128)} %param.6, s32[]{:T(128)} %constant.84.clone.1), dimensions={0}, to_apply=%region_1.0 | reduce | flops 1047552 | bytes 4198404 | tf_op jit(solution)/shard_map/reduce_sum | solution.py:78
  48.9 6.1 %gather_fusion.3 = s32[768,1024]{1,0:T(8,128)S(1)} fusion(s32[1024,1024]{0,1:T(8,128)} %copy.90, s32[1024]{0:T(1024)S(1)} %pad_clamp_fusion), kind=kCustom, calls=%fused_computation.5 | custom fusion | bytes 6294528 | tf_op jit(solution)/shard_map/jit(_take)/gather | solution.py:81
  55.1 3.1 %gather.34 = s32[1024,256,3]{0,2,1:T(4,128)} reshape(s32[1024,768]{0,1:T(8,128)S(1)} %bitcast.88) | data formatting | bytes 6291456 | tf_op jit(solution)/shard_map/jit(_take)/gather | solution.py:81
  58.2 3.4 %copy.110 = s32[1024,256,3]{1,0,2:T(8,128)S(1)} copy(s32[1024,256,3]{0,2,1:T(4,128)} %gather.34) | data formatting | bytes 6291456 | tf_op jit(solution)/shard_map/jit(_take)/gather | solution.py:81
  62.2 9.9 %all-reduce.1 = (f32[1024]{0:T(1024)S(1)}, f32[4,256]{1,0:T(4,128)S(1)}) all-reduce(f32[1024]{0:T(1024)S(1)} %convert_element_type.25, f32[4,256]{1,0:T(4,128)S(1)} %pad_maximum_fusion.1), channel_id=1, replica_groups=mesh['shot_0'=4,'shot_1'=8,'shot_2'=2,'det'=8] {'shot_0'}, use_global_device_ids=true, to_apply=%region_2.4 | all-reduce | flops 2048 | bytes 16384 | tf_op jit(solution)/shard_map/psum | solution.py:24
  72.2 30.8 %all-reduce = (f32[1024]{0:T(1024)S(1)}, f32[4,256]{1,0:T(4,128)S(1)}) all-reduce(f32[1024]{0:T(1024)S(1)} %get-tuple-element.14, f32[4,256]{1,0:T(4,128)S(1)} %get-tuple-element.15), channel_id=1, replica_groups=mesh['shot_0'=4,'shot_1'=8,'shot_2'=2,'det'=8] {'shot_1'}, use_global_device_ids=true, to_apply=%region_3.5 | all-reduce | flops 2048 | bytes 16384 | tf_op jit(solution)/shard_map/psum | solution.py:24
  103.0 5.2 %all-reduce.2 = (f32[1024]{0:T(1024)S(1)}, f32[4,256]{1,0:T(4,128)S(1)}) all-reduce(f32[1024]{0:T(1024)S(1)} %get-tuple-element.12, f32[4,256]{1,0:T(4,128)S(1)} %get-tuple-element.13), channel_id=1, replica_groups=mesh['shot_0'=4,'shot_1'=8,'shot_2'=2,'det'=8] {'shot_2'}, use_global_device_ids=true, to_apply=%region_4.6 | all-reduce | flops 2048 | bytes 16384 | tf_op jit(solution)/shard_map/psum | solution.py:24
  108.2 3.2 %gather_fusion.4 = f32[768]{0:T(1024)S(1)} fusion(f32[1024]{0:T(1024)S(1)} %get-tuple-element.16, s32[1024]{0:T(1024)S(1)} %pad_clamp_fusion), kind=kCustom, calls=%fused_computation.6 | custom fusion | bytes 9216 | tf_op jit(solution)/shard_map/jit(_take)/gather | solution.py:126
  111.6 0.6 gather_fusion.1
  112.3 0.6 gather_fusion
  113.1 2.3 %reduce_sum.72 = f32[34,2,128]{2,1,0:T(2,128)S(1)} reduce(f32[64,34,2,128]{3,2,1,0:T(2,128)} %all-to-all-done, f32[]{:T(128)} %constant.82.clone.1), dimensions={0}, to_apply=%region_0.2 | reduce | flops 548352 | bytes 2263044 | tf_op jit(solution)/shard_map/reduce_sum | solution.py:19
  115.4 0.7 fusion.23
  116.2 0.6 broadcast_in_dim.91
  116.8 10.0 %all-to-all-start.2 = ((f32[8,8,2]{1,2,0:T(2,128)}), f32[8,8,2]{1,2,0:T(2,128)S(1)}, u32[]{:S(2)}, u32[]{:S(2)}) async-start(f32[8,8,2]{1,2,0:T(2,128)} %broadcast_in_dim.91), calls=%async_computation.2 | async-start | bytes 16384 | tf_op jit(solution)/shard_map/all_to_all | solution.py:36
  126.9 0.7 gather_fusion.2
  127.7 1.0 select_multiply_fusion.1
  128.7 4.7 %all-to-all-done.2 = f32[8,8,2]{1,2,0:T(2,128)S(1)} async-done(((f32[8,8,2]{1,2,0:T(2,128)}), f32[8,8,2]{1,2,0:T(2,128)S(1)}, u32[]{:S(2)}, u32[]{:S(2)}) %all-to-all-start.2) | async-done | bytes 544 | tf_op jit(solution)/shard_map/all_to_all | solution.py:36
  133.3 11.0 %all-to-all-start.1 = ((f32[64,2,2,128]{3,2,1,0:T(2,128)}), f32[64,2,2,128]{3,2,1,0:T(2,128)S(1)}, u32[]{:S(2)}, u32[]{:S(2)}) async-start(f32[64,2,2,128]{3,2,1,0:T(2,128)} %select_multiply_fusion.1), calls=%async_computation.1 | async-start | bytes 262144 | tf_op jit(solution)/shard_map/all_to_all | solution.py:123
  144.6 0.6 fusion.17
  145.1 0.6 reshape.307
  145.8 8.8 %all-to-all-done.1 = f32[64,2,2,128]{3,2,1,0:T(2,128)S(1)} async-done(((f32[64,2,2,128]{3,2,1,0:T(2,128)}), f32[64,2,2,128]{3,2,1,0:T(2,128)S(1)}, u32[]{:S(2)}, u32[]{:S(2)}) %all-to-all-start.1) | async-done | bytes 131104 | tf_op jit(solution)/shard_map/all_to_all | solution.py:123
  154.6 0.7 copy.103
  (55 shorter events, 3.6 us)
Async XLA Ops:
  8.8 1.4 copy-start
  10.8 3.1 %copy-start.1 = (s32[1,26,2]{1,2,0:T(2,128)S(1)}, s32[1,26,2]{1,2,0:T(2,128)}, u32[]{:S(2)}) copy-start(s32[1,26,2]{1,2,0:T(2,128)} %param.7) | copy-start | bytes 628
  32.8 80.3 %all-to-all-start = ((f32[64,34,2,128]{3,2,1,0:T(2,128)}), f32[64,34,2,128]{3,2,1,0:T(2,128)}, u32[]{:S(2)}, u32[]{:S(2)}) async-start(f32[64,34,2,128]{3,2,1,0:T(2,128)} %bitcast.83), calls=%async_computation | async-start | bytes 4456448 | tf_op jit(solution)/shard_map/all_to_all | solution.py:18
  44.6 2.5 %copy-start.3 = (s32[1,26,2]{1,2,0:T(2,128)S(1)}, s32[1,26,2]{1,2,0:T(2,128)}, u32[]{:S(2)}) copy-start(s32[1,26,2]{1,2,0:T(2,128)} %param.8) | copy-start | bytes 628
  44.6 3.8 %copy-start.2 = (s32[1,256,3]{1,0,2:T(1,128)S(1)}, s32[1,256,3]{1,0,2:T(1,128)}, u32[]{:S(2)}) copy-start(s32[1,256,3]{1,0,2:T(1,128)} %param.9) | copy-start | bytes 9220
  116.8 16.6 %all-to-all-start.2 = ((f32[8,8,2]{1,2,0:T(2,128)}), f32[8,8,2]{1,2,0:T(2,128)S(1)}, u32[]{:S(2)}, u32[]{:S(2)}) async-start(f32[8,8,2]{1,2,0:T(2,128)} %broadcast_in_dim.91), calls=%async_computation.2 | async-start | bytes 16384 | tf_op jit(solution)/shard_map/all_to_all | solution.py:36
  133.3 21.3 %all-to-all-start.1 = ((f32[64,2,2,128]{3,2,1,0:T(2,128)}), f32[64,2,2,128]{3,2,1,0:T(2,128)S(1)}, u32[]{:S(2)}, u32[]{:S(2)}) async-start(f32[64,2,2,128]{3,2,1,0:T(2,128)} %select_multiply_fusion.1), calls=%async_computation.1 | async-start | bytes 262144 | tf_op jit(solution)/shard_map/all_to_all | solution.py:123
where the time goes:
time: 156 us; the launch traced here: 155 us
  blocking collectives  45.9 us (29%)
  local copies, waits for them, and re-layouts  42.5 us (27%)
  starting transfers between devices  32.7 us (21%)
  waiting for transfers between devices  13.5 us (9%)
  other arithmetic  11.5 us (7%)
  matrix products  8.12 us (5%)
    psum x3, blocking collectives, by_axis(): x = lax.psum(x, axis)  45.9 us
    gather x3, local copies, waits for them, and re-layouts, local(): jnp.take(events, triple_index.reshape(-1), axis=1).astype(jnp.float32)  12.6 us
    all_to_all x1, starting transfers between devices, sum_at_owner(): lax.all_to_all(tiles, axis, split_axis=0, concat_axis=0, tiled=True)  11.8 us
    all_to_all x1, starting transfers between devices, local(): lax.all_to_all(outgoing, SHOT, split_axis=0, concat_axis=2, tiled=True)  11 us
    all_to_all x1, starting transfers between devices, sent_to_all(): return lax.all_to_all(copies, axis, split_axis=0, concat_axis=0, tiled=True)  9.97 us
    all_to_all x1, waiting for transfers between devices, local(): lax.all_to_all(outgoing, SHOT, split_axis=0, concat_axis=2, tiled=True)  8.84 us
    dot_general x1, matrix products, local(): jnp.einsum('spi,spj->pij', first_columns, second_columns, preferred_eleme...  7.41 us
    unnamed x11, local copies, waits for them, and re-layouts  6.97 us
  transfers between devices with their start and end apart: 3, of which 2 were waited for; matrix products, arithmetic and copies ran while one was open for 17% of the time, Pallas kernels for 0%

commit v1 on v0

--- a/solution.py
+++ b/solution.py
@@ -21,7 +21,8 @@
 
 def by_axis(x, axes):
     for axis in axes:
-        x = lax.psum(x, axis)
+        right_arr = lax.all_gather(x, axis)
+        x = jnp.sum(right_arr, axis=0)
     return x
 
 

time: 156 us -> 219 us (1.40)
  blocking collectives: 45.9 us -> 108 us
    all_gather x0 -> x6, blocking collectives: none -> 108 us  [by_axis(): right_arr = lax.all_gather(x, axis)]
    psum x3 -> x0, blocking collectives: 45.9 us -> none  [by_axis(): x = lax.psum(x, axis)]
    unnamed x11 -> x15, local copies, waits for them, and re-layouts: 6.97 us -> 6.98 us
  transfers between devices with their start and end apart: 3 -> 3, of which waited for: 2 -> 2; matrix products, arithmetic and copies ran while one was open for 17% -> 13% of each run, Pallas kernels for 0% -> 0%
where the time goes in v1:
time: 219 us
  blocking collectives  108 us (49%)
  local copies, waits for them, and re-layouts  44.5 us (20%)
  starting transfers between devices  31.4 us (14%)
  waiting for transfers between devices  13.5 us (6%)
  other arithmetic  12.1 us (6%)
  matrix products  8.12 us (4%)
    all_gather x6, blocking collectives, by_axis(): right_arr = lax.all_gather(x, axis)  108 us
    gather x3, local copies, waits for them, and re-layouts, local(): jnp.take(events, triple_index.reshape(-1), axis=1).astype(jnp.float32)  12.6 us
    all_to_all x1, starting transfers between devices, sum_at_owner(): lax.all_to_all(tiles, axis, split_axis=0, concat_axis=0, tiled=True)  11.8 us
    all_to_all x1, starting transfers between devices, sent_to_all(): return lax.all_to_all(copies, axis, split_axis=0, concat_axis=0, tiled=True)  9.94 us
    all_to_all x1, starting transfers between devices, local(): lax.all_to_all(outgoing, SHOT, split_axis=0, concat_axis=2, tiled=True)  9.73 us
    all_to_all x1, waiting for transfers between devices, local(): lax.all_to_all(outgoing, SHOT, split_axis=0, concat_axis=2, tiled=True)  8.84 us
    dot_general x1, matrix products, local(): jnp.einsum('spi,spj->pij', first_columns, second_columns, preferred_eleme...  7.41 us
    unnamed x15, local copies, waits for them, and re-layouts  6.98 us
  transfers between devices with their start and end apart: 3, of which 2 were waited for; matrix products, arithmetic and copies ran while one was open for 13% of the time, Pallas kernels for 0%

profile of v1, /device:TPU:1, one launch (start us, length us, event | category | flops | bytes accessed | tf_op | source)
XLA Modules:
  0.0 218.5 jit_solution(3087502450818276889)
XLA Ops:
  0.6 5.4 %copy.90 = s32[1024,1024]{0,1:T(8,128)} copy(s32[1024,1024]{1,0:T(8,128)} %param.6) | data formatting | bytes 8388608 | tf_op args[0]
  6.0 2.8 %convert_element_type.34 = bf16[1024,1024]{0,1:T(8,128)(2,1)S(1)} convert(s32[1024,1024]{0,1:T(8,128)} %copy.90) | non-fusion elementwise | flops 1048576 | bytes 6291456 | tf_op jit(solution)/shard_map/convert_element_type | solution.py:77
  8.8 1.3 copy-done
  10.1 0.7 fusion.24
  10.8 3.0 %copy.92 = bf16[1024,8,128]{2,0,1:T(8,128)(2,1)S(1)} copy(bf16[1024,8,128]{0,2,1:T(8,128)(2,1)} %bitcast.90) | data formatting | bytes 4194304 | tf_op jit(solution)/shard_map/reshape | solution.py:78
  13.9 4.5 %gather_fusion.6 = bf16[26,1024,128]{2,1,0:T(8,128)(2,1)} fusion(bf16[1024,8,128]{2,0,1:T(8,128)(2,1)S(1)} %copy.92, s32[1024]{0:T(1024)S(1)} %get-tuple-element.36), kind=kCustom, calls=%fused_computation.1.clone | custom fusion | bytes 13631592 | tf_op jit(solution)/shard_map/jit(_take)/gather | solution.py:100
  18.5 4.6 %gather_fusion.5 = bf16[26,1024,128]{2,1,0:T(8,128)(2,1)} fusion(bf16[1024,8,128]{2,0,1:T(8,128)(2,1)S(1)} %copy.92, s32[1024]{0:T(1024)S(1)} %get-tuple-element.37), kind=kCustom, calls=%fused_computation.clone | custom fusion | bytes 13631592 | tf_op jit(solution)/shard_map/jit(_take)/gather | solution.py:99
  23.1 7.4 %fusion = f32[26,128,128]{2,1,0:T(8,128)S(1)} fusion(bf16[26,1024,128]{2,1,0:T(8,128)(2,1)} %gather_fusion.6, bf16[26,1024,128]{2,1,0:T(8,128)(2,1)} %gather_fusion.5, pred[26]{0:T(512)(128)(4,1)S(1)} %get-tuple-element.32, pred[26]{0:T(512)(128)(4,1)S(1)} %get-tuple-element.18), kind=kOutput, calls=%fused_computation.7 | convolution fusion | flops 879230976 | bytes 15335476 | tf_op jit(solution)/shard_map/spi,spj->pij/dot_general | solution.py:101
  30.7 2.1 copy.115
  32.8 11.8 %all-to-all-start = ((f32[64,34,2,128]{3,2,1,0:T(2,128)}), f32[64,34,2,128]{3,2,1,0:T(2,128)}, u32[]{:S(2)}, u32[]{:S(2)}) async-start(f32[64,34,2,128]{3,2,1,0:T(2,128)} %bitcast.86), calls=%async_computation | async-start | bytes 4456448 | tf_op jit(solution)/shard_map/all_to_all | solution.py:18
  44.6 2.5 %reduce_sum.127 = s32[1024]{0:T(1024)S(1)} reduce(s32[1024,1024]{1,0:T(8,128)} %param.6, s32[]{:T(128)} %constant.84.clone.1), dimensions={0}, to_apply=%region_1.0 | reduce | flops 1047552 | bytes 4198404 | tf_op jit(solution)/shard_map/reduce_sum | solution.py:79
  47.1 10.9 %all-gather = f32[4096]{0:T(1024)S(1)} all-gather(f32[1024]{0:T(1024)S(1)} %convert_element_type.35), channel_id=2, replica_groups=mesh['shot_0'=4,'shot_1'=8,'shot_2'=2,'det'=8] {'shot_0'}, dimensions={0}, use_global_device_ids=true | all-gather | bytes 20480 | tf_op jit(solution)/shard_map/all_gather | solution.py:24
  58.2 50.4 %all-gather.1 = f32[8192]{0:T(1024)S(1)} all-gather(f32[1024]{0:T(1024)S(1)} %reduce_sum.128), channel_id=3, replica_groups=mesh['shot_0'=4,'shot_1'=8,'shot_2'=2,'det'=8] {'shot_1'}, dimensions={0}, use_global_device_ids=true | all-gather | bytes 36864 | tf_op jit(solution)/shard_map/all_gather | solution.py:24
  108.6 7.6 %all-gather.2 = f32[2048]{0:T(1024)S(1)} all-gather(f32[1024]{0:T(1024)S(1)} %reduce_sum.129), channel_id=4, replica_groups=mesh['shot_0'=4,'shot_1'=8,'shot_2'=2,'det'=8] {'shot_2'}, dimensions={0}, use_global_device_ids=true | all-gather | bytes 12288 | tf_op jit(solution)/shard_map/all_gather | solution.py:24
  117.7 0.7 copy.102
  118.8 6.1 %gather_fusion.3 = s32[768,1024]{1,0:T(8,128)S(1)} fusion(s32[1024,1024]{0,1:T(8,128)} %copy.90, s32[1024]{0:T(1024)S(1)} %pad_clamp_fusion), kind=kCustom, calls=%fused_computation.5 | custom fusion | bytes 6294528 | tf_op jit(solution)/shard_map/jit(_take)/gather | solution.py:82
  125.0 3.2 %gather_fusion.4 = f32[768]{0:T(1024)S(1)} fusion(f32[1024]{0:T(1024)S(1)} %reduce_sum.130, s32[1024]{0:T(1024)S(1)} %pad_clamp_fusion), kind=kCustom, calls=%fused_computation.6 | custom fusion | bytes 9216 | tf_op jit(solution)/shard_map/jit(_take)/gather | solution.py:127
  129.0 0.8 copy.107
  129.8 3.1 %gather.34 = s32[1024,256,3]{0,2,1:T(4,128)} reshape(s32[1024,768]{0,1:T(8,128)S(1)} %bitcast.91) | data formatting | bytes 6291456 | tf_op jit(solution)/shard_map/jit(_take)/gather | solution.py:82
  132.9 3.4 %copy.110 = s32[1024,256,3]{1,0,2:T(8,128)S(1)} copy(s32[1024,256,3]{0,2,1:T(4,128)} %gather.34) | data formatting | bytes 6291456 | tf_op jit(solution)/shard_map/jit(_take)/gather | solution.py:82
  136.9 9.8 %all-gather.6 = f32[4,4,256]{2,1,0:T(4,128)S(1)} all-gather(f32[1,4,256]{2,1,0:T(4,128)S(1)} %maximum_bitcast_fusion), channel_id=5, replica_groups=mesh['shot_0'=4,'shot_1'=8,'shot_2'=2,'det'=8] {'shot_0'}, dimensions={0}, use_global_device_ids=true | all-gather | bytes 20480 | tf_op jit(solution)/shard_map/all_gather | solution.py:24
  146.7 18.3 %all-gather.7 = f32[8,4,256]{2,1,0:T(4,128)S(1)} all-gather(f32[1,4,256]{2,1,0:T(4,128)S(1)} %bitcast.97), channel_id=6, replica_groups=mesh['shot_0'=4,'shot_1'=8,'shot_2'=2,'det'=8] {'shot_1'}, dimensions={0}, use_global_device_ids=true | all-gather | bytes 36864 | tf_op jit(solution)/shard_map/all_gather | solution.py:24
  165.0 11.1 %all-gather.8 = f32[2,4,256]{2,1,0:T(4,128)S(1)} all-gather(f32[1,4,256]{2,1,0:T(4,128)S(1)} %bitcast.96), channel_id=7, replica_groups=mesh['shot_0'=4,'shot_1'=8,'shot_2'=2,'det'=8] {'shot_2'}, dimensions={0}, use_global_device_ids=true | all-gather | bytes 12288 | tf_op jit(solution)/shard_map/all_gather | solution.py:24
  177.6 2.3 %reduce_sum.126 = f32[34,2,128]{2,1,0:T(2,128)S(1)} reduce(f32[64,34,2,128]{3,2,1,0:T(2,128)} %all-to-all-done, f32[]{:T(128)} %constant.82.clone.1), dimensions={0}, to_apply=%region_0.2 | reduce | flops 548352 | bytes 2263044 | tf_op jit(solution)/shard_map/reduce_sum | solution.py:19
  179.8 0.7 fusion.23
  181.2 9.9 %all-to-all-start.2 = ((f32[8,8,2]{1,2,0:T(2,128)}), f32[8,8,2]{1,2,0:T(2,128)S(1)}, u32[]{:S(2)}, u32[]{:S(2)}) async-start(f32[8,8,2]{1,2,0:T(2,128)} %broadcast_in_dim.91), calls=%async_computation.2 | async-start | bytes 16384 | tf_op jit(solution)/shard_map/all_to_all | solution.py:37
  191.3 0.7 gather_fusion.2
  192.1 1.0 select_multiply_fusion.1
  193.1 4.7 %all-to-all-done.2 = f32[8,8,2]{1,2,0:T(2,128)S(1)} async-done(((f32[8,8,2]{1,2,0:T(2,128)}), f32[8,8,2]{1,2,0:T(2,128)S(1)}, u32[]{:S(2)}, u32[]{:S(2)}) %all-to-all-start.2) | async-done | bytes 544 | tf_op jit(solution)/shard_map/all_to_all | solution.py:37
  197.7 9.7 %all-to-all-start.1 = ((f32[64,2,2,128]{3,2,1,0:T(2,128)}), f32[64,2,2,128]{3,2,1,0:T(2,128)S(1)}, u32[]{:S(2)}, u32[]{:S(2)}) async-start(f32[64,2,2,128]{3,2,1,0:T(2,128)} %select_multiply_fusion.1), calls=%async_computation.1 | async-start | bytes 262144 | tf_op jit(solution)/shard_map/all_to_all | solution.py:124
  209.0 8.8 %all-to-all-done.1 = f32[64,2,2,128]{3,2,1,0:T(2,128)S(1)} async-done(((f32[64,2,2,128]{3,2,1,0:T(2,128)}), f32[64,2,2,128]{3,2,1,0:T(2,128)S(1)}, u32[]{:S(2)}, u32[]{:S(2)}) %all-to-all-start.1) | async-done | bytes 131104 | tf_op jit(solution)/shard_map/all_to_all | solution.py:124
  217.8 0.7 copy.103
  (69 shorter events, 7.5 us)
Async XLA Ops:
  8.8 1.4 copy-start
  10.8 3.1 %copy-start.2 = (s32[1,26,2]{1,2,0:T(2,128)S(1)}, s32[1,26,2]{1,2,0:T(2,128)}, u32[]{:S(2)}) copy-start(s32[1,26,2]{1,2,0:T(2,128)} %param.7) | copy-start | bytes 628
  32.8 144.7 %all-to-all-start = ((f32[64,34,2,128]{3,2,1,0:T(2,128)}), f32[64,34,2,128]{3,2,1,0:T(2,128)}, u32[]{:S(2)}, u32[]{:S(2)}) async-start(f32[64,34,2,128]{3,2,1,0:T(2,128)} %bitcast.86), calls=%async_computation | async-start | bytes 4456448 | tf_op jit(solution)/shard_map/all_to_all | solution.py:18
  44.6 13.4 %copy-start.4 = (s32[1,26,2]{1,2,0:T(2,128)S(1)}, s32[1,26,2]{1,2,0:T(2,128)}, u32[]{:S(2)}) copy-start(s32[1,26,2]{1,2,0:T(2,128)} %param.8) | copy-start | bytes 628
  44.6 73.8 %copy-start.3 = (s32[1,256,3]{1,0,2:T(1,128)S(1)}, s32[1,256,3]{1,0,2:T(1,128)}, u32[]{:S(2)}) copy-start(s32[1,256,3]{1,0,2:T(1,128)} %param.9) | copy-start | bytes 9220
  136.6 40.7 %copy-start.5 = (s32[128,1]{0,1:T(1,128)S(1)}, s32[128,1]{0,1:T(1,128)}, u32[]{:S(2)}) copy-start(s32[128,1]{0,1:T(1,128)} %reshape.314) | copy-start | bytes 1540
  136.6 55.5 %copy-start.1 = (f32[64,2]{1,0:T(8,128)S(1)}, f32[64,2]{1,0:T(8,128)}, u32[]{:S(2)}) copy-start(f32[64,2]{1,0:T(8,128)} %copy.102) | copy-start | bytes 1540
  181.2 16.5 %all-to-all-start.2 = ((f32[8,8,2]{1,2,0:T(2,128)}), f32[8,8,2]{1,2,0:T(2,128)S(1)}, u32[]{:S(2)}, u32[]{:S(2)}) async-start(f32[8,8,2]{1,2,0:T(2,128)} %broadcast_in_dim.91), calls=%async_computation.2 | async-start | bytes 16384 | tf_op jit(solution)/shard_map/all_to_all | solution.py:37
  197.7 20.1 %all-to-all-start.1 = ((f32[64,2,2,128]{3,2,1,0:T(2,128)}), f32[64,2,2,128]{3,2,1,0:T(2,128)S(1)}, u32[]{:S(2)}, u32[]{:S(2)}) async-start(f32[64,2,2,128]{3,2,1,0:T(2,128)} %select_multiply_fusion.1), calls=%async_computation.1 | async-start | bytes 262144 | tf_op jit(solution)/shard_map/all_to_all | solution.py:124
